TPU v7x, 256 devices: a whole 4x4x8 slice. The times are simulated.
256 devices in a mesh: group: 8 (over z), mp: 32 (over y, x, core).
Axes of the slice: x: 4, y: 4, z: 8, core: 2. Of those that a mesh axis runs over, the one named last changes fastest.
Arguments:
- option_latent_states: bfloat16 [2048, 8192], P('group', 'mp'), may hold values from -6 to 6
- mixer_scaling_factor: bfloat16 [1, 8192], P(None, 'mp'), may hold values from 0.099609375 to 1.8984375
- question_mapping_matrix: bfloat16 [8192, 8192], P(None, 'mp'), may hold values from -0.0625 to 0.0625
- lookup_content_matrix: bfloat16 [8192, 2048], P(None, 'mp'), may hold values from -0.0625 to 0.0625
- final_mapping_matrix: bfloat16 [8192, 8192], P('mp'), may hold values from -0.125 to 0.125
- payoff_readout_vector: bfloat16 [8192], P('mp'), may hold values from -0.0625 to 0.0625
- shared_trie_memo: bfloat16 [2, 512, 128, 1024], P(None, ('group', 'mp')), may hold values from -100 to 100
- option_route_pages: int32 [128, 32], P('group'), may hold values from 0 to 63, as said below
- option_page_tally: int32 [128], P('group'), may hold values from 1 to 32, as said below
- option_token_span: int32 [128], P('group'), may hold values from 1 to 16
- retained_pages: int32 [512], P(('group', 'mp')), may hold values from 0 to 1
- growth_place_mapping: int32 [768], P(('group', 'mp')), may hold values from 0 to 15, as said below
Outputs:
- scored_rows: bfloat16 [2048, 8192], P('group', 'mp')
- rewards: float32 [128], P('group')
- expanded: bfloat16 [2, 768, 128, 1024], P(None, ('group', 'mp'))
Inputs may be any that keep to these rules, and one draw needn't show every extreme that they name: `option_route_pages`: the t-th listed block of a candidate is one of t * 2 to (t + 1) * 2 - 1; entries at or past option_page_tally are not read. `option_page_tally`: among the 16 candidates of each group index one lists all 32 blocks. `growth_place_mapping`: for every mp index, every survivor of every group index fills some slot.
All inputs are finite; a program needn't handle non-finite values.
Results may differ from a plain program's by a relative error of at most 0.005.
The roundings to bfloat16 on the way count: a program that leaves them out, or rounds other values in their place, can miss the bound.
Values may be sent and summed in bfloat16 or wider, within the bound.
No kernel may reach another device: no remote copies, remote signals or barrier semaphores. Data moves between devices by JAX's collectives and lax.ppermute only.
A program may use at most 128 MiB of HBM per device.

v0:
```python
import jax
import jax.numpy as jnp
from jax import lax
from jax.sharding import Mesh
from jax.sharding import PartitionSpec as P

D = 8192
HEADS = 64
KVH = 8
HD = 128
BLK = 128
STEP = 16
MP = ("mp_0", "mp_1", "mp_2")
GROUP_MP = ("group", "mp_0", "mp_1", "mp_2")
epsilon = 1e-06
masked_value = -1e30


def sent_together(arrays, axis, dim, along):
    ends, at = ([], 0)
    for a in arrays[:-1]:
        at += a.shape[along]
        ends.append(at)
    both = jnp.concatenate(arrays, axis=along)
    return tuple(jnp.split(lax.all_gather(both, axis, axis=dim, tiled=True), ends, axis=along))


def in_order(tiles, dim):
    lengths = list(tiles.shape[1:])
    lengths[dim] *= tiles.shape[0]
    return jnp.moveaxis(tiles, 0, dim).reshape(lengths)


def from_everyone(x, axis):
    copies = jnp.broadcast_to(x, (lax.axis_size(axis), *x.shape))
    return lax.all_to_all(copies, axis, split_axis=0, concat_axis=0, tiled=True)


def collect(x, axis, dim):
    return in_order(from_everyone(x, axis), dim)


def split_up(x, dim, count):
    before, after = (x.shape[:dim], x.shape[dim + 1 :])
    return jnp.moveaxis(x.reshape(*before, count, -1, *after), dim, 0)


def scatter_pairs(x, chips, core, dim):
    sizes = (lax.axis_size(chips), lax.axis_size(core))
    tiles = split_up(x, dim, sizes[0] * sizes[1])
    inside = tiles.shape[1:]
    tiles = tiles.reshape(*sizes, *inside).swapaxes(0, 1).reshape(-1, *inside)
    tiles = lax.psum_scatter(tiles, core, scatter_dimension=0, tiled=True)
    return lax.psum_scatter(tiles, chips, scatter_dimension=0, tiled=True)[0]


def over_copies(x, axis):
    everything = from_everyone(x, axis)
    return jnp.sum(everything, axis=0)


def local(
    option_latent_states,
    mixer_scaling_factor,
    question_mapping_matrix,
    lookup_content_matrix,
    final_mapping_matrix,
    payoff_readout_vector,
    shared_trie_memo,
    option_route_pages,
    option_page_tally,
    option_token_span,
    retained_pages,
    growth_place_mapping,
):
    width_mp = lax.axis_size(MP)
    my_index = lax.axis_index(MP)
    received = lax.all_to_all(
        option_latent_states, "group", split_axis=0, concat_axis=0, tiled=True
    )
    row_total = received.shape[0]
    cand_here = row_total // STEP
    heads_here = question_mapping_matrix.shape[1] // HD
    group_size = HEADS // KVH
    pair_head = my_index * heads_here // group_size
    score_scale = HD ** (-0.5)
    row_piece, gain_piece = sent_together((received, mixer_scaling_factor), MP, 1, 0)
    piece_wide = row_piece.astype(jnp.float32)
    scaled = (piece_wide * gain_piece.astype(jnp.float32)).astype(jnp.bfloat16)
    query_sum = jnp.dot(scaled, question_mapping_matrix, preferred_element_type=jnp.float32)
    pair_sum = lax.dot_general(
        lookup_content_matrix, scaled, (((0,), (1,)), ((), ())), preferred_element_type=jnp.float32
    )
    square_sum = jnp.sum(piece_wide * piece_wide, axis=1)
    query_sum, pair_sum, square_sum = (query_sum, pair_sum, square_sum)
    inv_rms = lax.rsqrt(square_sum / D + epsilon)
    queries = (query_sum * inv_rms[:, None]).astype(jnp.bfloat16)
    pair_part = (pair_sum * inv_rms[None, :]).astype(jnp.bfloat16)
    fresh_pairs = collect(pair_part, MP, 0)
    fresh_keys = lax.dynamic_slice_in_dim(fresh_pairs, pair_head * HD, HD, 0).reshape(
        HD, cand_here, STEP
    )
    fresh_values = lax.dynamic_slice_in_dim(fresh_pairs, (KVH + pair_head) * HD, HD, 0).reshape(
        HD, cand_here, STEP
    )
    own_queries = queries.reshape(cand_here, STEP, heads_here, HD)
    position = jnp.arange(STEP, dtype=jnp.int32)
    own_mask = (position[None, None, :] <= position[None, :, None]) & (
        position[None, None, :] < option_token_span[:, None, None]
    )
    own_score = (
        jnp.einsum("csjd,dcu->jcsu", own_queries, fresh_keys, preferred_element_type=jnp.float32)
        * score_scale
    )
    own_score = jnp.where(own_mask[None], own_score, masked_value)
    own_top = jnp.max(own_score, axis=-1).reshape(heads_here, row_total)
    pool_here = shared_trie_memo.shape[1]
    pool_group = pool_here * width_mp
    listed = (
        jnp.arange(option_route_pages.shape[1], dtype=jnp.int32)[None, :]
        < option_page_tally[:, None]
    )
    member = jnp.any(
        (option_route_pages[:, :, None] == jnp.arange(pool_group, dtype=jnp.int32)[None, None, :])
        & listed[:, :, None],
        axis=1,
    )
    spread = shared_trie_memo.reshape(2, pool_here, BLK, KVH, 1, HD)
    spread = jnp.broadcast_to(spread, (2, pool_here, BLK, KVH, width_mp // KVH, HD)).reshape(
        2, pool_here, BLK, width_mp, HD
    )
    head_pool = lax.all_to_all(spread, MP, split_axis=3, concat_axis=1, tiled=True)
    path_keys = head_pool[0].reshape(pool_group * BLK, HD)
    path_values = head_pool[1].reshape(pool_group * BLK, HD)
    path_mask = jnp.broadcast_to(
        member[:, None, :, None], (cand_here, STEP, pool_group, BLK)
    ).reshape(row_total, pool_group * BLK)
    my_queries = queries.reshape(row_total, heads_here, HD)
    sum_list = []
    total_list = []
    top_list = []
    for head_index in range(heads_here):
        head_score = (
            jnp.einsum(
                "rd,pd->rp",
                my_queries[:, head_index],
                path_keys,
                preferred_element_type=jnp.float32,
            )
            * score_scale
        )
        head_score = jnp.where(path_mask, head_score, masked_value)
        head_top = jnp.maximum(jnp.max(head_score, axis=-1), own_top[head_index])
        head_mass = jnp.where(path_mask, jnp.exp(head_score - head_top[:, None]), 0.0)
        sum_list.append(
            jnp.dot(head_mass.astype(jnp.bfloat16), path_values, preferred_element_type=jnp.float32)
        )
        total_list.append(jnp.sum(head_mass, axis=-1))
        top_list.append(head_top)
    path_sum = jnp.stack(sum_list)
    path_total = jnp.stack(total_list)
    row_top = jnp.stack(top_list)
    top_grid = row_top.reshape(heads_here, cand_here, STEP)[..., None]
    own_mass = jnp.where(own_mask[None], jnp.exp(own_score - top_grid), 0.0)
    own_sum = jnp.einsum(
        "jcsu,dcu->jcsd",
        own_mass.astype(jnp.bfloat16),
        fresh_values,
        preferred_element_type=jnp.float32,
    ).reshape(heads_here, row_total, HD)
    own_total = jnp.sum(own_mass, axis=-1).reshape(heads_here, row_total)
    attended = ((path_sum + own_sum) / (path_total + own_total)[..., None]).astype(jnp.bfloat16)
    partial_value = jnp.einsum(
        "jrd,jdf->rf",
        attended,
        final_mapping_matrix.reshape(heads_here, HD, D),
        preferred_element_type=jnp.float32,
    )
    projected = scatter_pairs(partial_value, ("mp_0", "mp_1"), "mp_2", 1)
    live_rows = (position[None, :] < option_token_span[:, None]).reshape(row_total)
    scored_rows = (projected * live_rows[:, None].astype(jnp.float32)).astype(jnp.bfloat16)
    last_row = (position[None, :] == option_token_span[:, None] - 1).astype(jnp.float32)
    last_values = jnp.sum(projected.reshape(cand_here, STEP, -1) * last_row[:, :, None], axis=1)
    partial_reward = jnp.sum(
        last_values * payoff_readout_vector.astype(jnp.float32)[None, :], axis=1
    )
    rewards = over_copies(partial_reward, MP)
    gathered_elements = jnp.take(shared_trie_memo, retained_pages, axis=1)
    gathered = lax.all_gather(gathered_elements, "group", axis=1, tiled=True)
    expanded = jnp.take(gathered, growth_place_mapping, axis=1)
    return (scored_rows, rewards, expanded)


def solution(mesh):
    split = Mesh(
        mesh.devices.reshape(mesh.shape["group"], 4, 4, 2), ("group", "mp_0", "mp_1", "mp_2")
    )
    in_specs = (
        P("group", MP),
        P(None, MP),
        P(None, MP),
        P(None, MP),
        P(MP, None),
        P(MP),
        P(None, GROUP_MP, None, None),
        P("group", None),
        P("group"),
        P("group"),
        P(GROUP_MP),
        P(GROUP_MP),
    )
    out_specs = (P("group", MP), P("group"), P(None, GROUP_MP, None, None))
    return jax.shard_map(local, mesh=split, in_specs=in_specs, out_specs=out_specs, check_vma=False)
```

profile of v0, /device:TPU:1, one launch (start us, length us, event | category | flops | bytes accessed | tf_op | source)
XLA Modules:
  0.0 321.8 jit_solution(12386661473913503255)
XLA Ops:
  8.1 16.9 %all_to_all.38 = bf16[8,32,256]{2,1,0:T(8,128)(2,1)S(1)} all-to-all(bf16[8,32,256]{2,1,0:T(8,128)(2,1)} %bitcast.140), channel_id=1, replica_groups=mesh['group'=8,'mp_0'=4,'mp_1'=4,'mp_2'=2] {'group'}, dimensions={0} | all-to-all | bytes 262144 | tf_op jit(solution)/shard_map/all_to_all | solution.py:78
  25.0 1.3 pad_maximum_fusion
  26.3 0.3 copy_bitcast_fusion.1
  26.6 3.2 %broadcast_in_dim.94 = bf16[2,2,128,8,4,128]{5,2,1,0,4,3:T(8,128)(2,1)} broadcast(bf16[2,2,128,8,128]{4,2,1,0,3:T(8,128)(2,1)S(1)} %copy_bitcast_fusion.1), dimensions={0,1,2,3,5} | broadcast | bytes 5242880 | tf_op jit(solution)/shard_map/broadcast_in_dim | solution.py:129
  29.8 9.4 %all-to-all-start.1 = ((bf16[2,2,128,32,128]{4,2,1,0,3:T(8,128)(2,1)}), bf16[2,2,128,32,128]{4,2,1,0,3:T(8,128)(2,1)}, u32[]{:S(2)}, u32[]{:S(2)}) async-start(bf16[2,2,128,32,128]{4,2,1,0,3:T(8,128)(2,1)} %bitcast.123), calls=%async_computation.1 | async-start | bytes 8388608 | tf_op jit(solution)/shard_map/all_to_all | solution.py:132
  39.4 6.4 %copy.103 = bf16[8192,128,2]{1,0,2:T(8,128)(2,1)} copy(bf16[8192,128,2]{0,1,2:T(8,128)(2,1)} %bitcast.132) | data formatting | bytes 8388608 | tf_op jit(solution)/shard_map/jrd,jdf->rf/dot_general | solution.py:173
  45.7 0.1 iota_compare_fusion.4
  45.8 0.2 fusion.47
  46.0 0.1 fusion.61
  46.1 0.1 broadcast_and_fusion
  46.2 45.6 %all-to-all-done.1 = bf16[2,2,128,32,128]{4,2,1,0,3:T(8,128)(2,1)} async-done(((bf16[2,2,128,32,128]{4,2,1,0,3:T(8,128)(2,1)}), bf16[2,2,128,32,128]{4,2,1,0,3:T(8,128)(2,1)}, u32[]{:S(2)}, u32[]{:S(2)}) %all-to-all-start.1) | async-done | bytes 4194336 | tf_op jit(solution)/shard_map/all_to_all | solution.py:132
  91.8 2.5 copy.135
  94.3 2.3 fusion.64
  96.6 18.1 %all-gather.3.cloned.1.call-done = bf16[257,8192]{1,0:T(8,128)(2,1)} async-done(((bf16[257,256]{1,0:T(8,128)(2,1)}), bf16[257,8192]{1,0:T(8,128)(2,1)}) %all-gather.3.cloned.1.call-update) | async-done | bytes 4210704 | tf_op jit(solution)/shard_map/all_gather | solution.py:25
  114.7 3.1 fusion.3
  117.8 0.9 slice_convert_fusion
  118.7 3.6 %fusion.40 = bf16[64,256]{1,0:T(8,128)(2,1)S(1)} fusion(bf16[8192,64]{0,1:T(8,128)(2,1)S(1)} %copy-done.10, f32[8192]{0:T(1024)S(1)} %bitcast.147, bf16[257,8192]{1,0:T(8,128)(2,1)} %all-gather.3.cloned.1.call-done, f32[256]{0:T(256)S(1)} %add_rsqrt_fusion), kind=kOutput, calls=%fused_computation.36 | convolution fusion | flops 274759680 | bytes 5309440 | tf_op jit(solution)/shard_map/dot_general | solution.py:91
  122.3 1.1 broadcast_in_dim.97
  123.4 5.5 %all-to-all-start.2 = ((bf16[32,64,256]{2,1,0:T(8,128)(2,1)}), bf16[32,64,256]{2,1,0:T(8,128)(2,1)}, u32[]{:S(2)}, u32[]{:S(2)}) async-start(bf16[32,64,256]{2,1,0:T(8,128)(2,1)} %broadcast_in_dim.97), calls=%async_computation.2 | async-start | bytes 2097152 | tf_op jit(solution)/shard_map/all_to_all | solution.py:36
  128.9 0.2 reduce-scatter.5.cloned.1.call-start
  129.1 5.4 %fusion.25 = bf16[256,256]{0,1:T(8,128)(2,1)S(1)} fusion(bf16[8192,256]{1,0:T(8,128)(2,1)} %param.14, f32[8192]{0:T(1024)S(1)} %bitcast.148, bf16[257,8192]{1,0:T(8,128)(2,1)} %all-gather.3.cloned.1.call-done, f32[256]{0:T(256)S(1)} %add_rsqrt_fusion), kind=kOutput, calls=%fused_computation.31 | convolution fusion | flops 1080164352 | bytes 8553472 | tf_op jit(solution)/shard_map/dot_general | solution.py:90
  134.5 0.1 copy.95
  134.6 0.7 reshape.267
  135.3 0.6 broadcast_in_dim.92
  135.9 7.5 %fusion.68 = (f32[256]{0:T(256)S(1)}, f32[256,8192]{1,0:T(8,128)}) fusion(bf16[8192,128]{1,0:T(8,128)(2,1)} %bitcast.135, bf16[256,2,128]{0,2,1:T(8,128)(2,1)S(1)} %bitcast.141, pred[32,8,64,128]{3,2,1,0:T(32,128)(4,1)S(1)} %bitcast.127), kind=kOutput, calls=%fused_computation.91 | convolution fusion | flops 543162112 | bytes 12649472 | tf_op jit(solution)/shard_map/rd,pd->rp/dot_general | solution.py:144
  143.4 0.1 reduce_max.34
  143.5 7.5 %fusion.66 = (f32[256]{0:T(256)S(1)}, f32[256,8192]{1,0:T(8,128)}) fusion(bf16[8192,128]{1,0:T(8,128)(2,1)} %bitcast.136, bf16[256,2,128]{0,2,1:T(8,128)(2,1)S(1)} %bitcast.142, pred[32,8,64,128]{3,2,1,0:T(32,128)(4,1)S(1)} %bitcast.128), kind=kOutput, calls=%fused_computation.89 | convolution fusion | flops 543162112 | bytes 12649472 | tf_op jit(solution)/shard_map/rd,pd->rp/dot_general | solution.py:144
  151.0 0.1 reduce_max.35
  151.1 0.9 constant_dynamic-slice_fusion
  152.0 0.7 copy.94
  152.7 1.4 fusion.67
  154.1 0.6 squeeze.20
  154.8 1.3 max.34
  156.0 0.6 squeeze.22
  156.7 0.7 max.35
  157.4 7.5 %fusion.28 = f32[1,256,128]{2,1,0:T(8,128)} fusion(bf16[8192,128]{1,0:T(8,128)(2,1)} %bitcast.133, f32[256,8192]{1,0:T(8,128)} %get-tuple-element.37, f32[256]{0:T(256)} %max.34, pred[32,8,64,128]{3,2,1,0:T(32,128)(4,1)S(1)} %bitcast.129), kind=kOutput, calls=%fused_computation.32 | convolution fusion | flops 543162368 | bytes 12715008 | tf_op jit(solution)/shard_map/dot_general | solution.py:156
  164.9 7.6 %fusion.4 = (f32[256]{0:T(256)}, f32[256]{0:T(256)}) fusion(f32[256,8192]{1,0:T(8,128)S(1)} %copy-done.1, f32[256]{0:T(256)S(1)} %copy-done.4, pred[32,8,64,128]{3,2,1,0:T(32,128)(4,1)S(1)} %bitcast.130, f32[256,8192]{1,0:T(8,128)} %get-tuple-element.33, f32[256]{0:T(256)S(1)} %max.35), kind=kLoop, calls=%fused_computation.12 | loop fusion | flops 12582400 | bytes 18878464 | tf_op jit(solution)/shard_map/reduce_sum | solution.py:158
  172.5 3.7 %fusion.31 = f32[1,256,128]{2,1,0:T(8,128)} fusion(bf16[8192,128]{1,0:T(8,128)(2,1)S(1)} %bitcast.134, f32[256,8192]{1,0:T(8,128)S(1)} %bitcast.126, f32[256]{0:T(256)S(1)} %max.35, pred[32,8,64,128]{3,2,1,0:T(32,128)(4,1)S(1)} %bitcast.131), kind=kOutput, calls=%fused_computation.33 | convolution fusion | flops 543162368 | bytes 12715008 | tf_op jit(solution)/shard_map/dot_general | solution.py:156
  176.3 0.1 fusion.48
  176.4 0.1 reshape.270
  176.5 0.1 copy.98
  176.6 0.2 convolution_bitcast_fusion
  176.9 0.7 maximum_add_fusion.1
  177.5 1.1 fusion.44
  178.7 3.5 %fusion.51 = f32[256,32,256,1]{2,0,1,3:T(8,128)S(1)} fusion(bf16[32,256,128,2]{2,1,0,3:T(8,128)(2,1)} %bitcast.120, bf16[2,256,128]{2,1,0:T(8,128)(2,1)S(1)} %fusion.44), kind=kOutput, calls=%fused_computation.52 | convolution fusion | flops 1073741824 | bytes 12713984 | tf_op jit(solution)/shard_map/jrd,jdf->rf/dot_general | solution.py:173
  182.1 3.8 %copy.105 = f32[2,16,256,256]{3,2,1,0:T(8,128)} copy(f32[2,16,256,256]{3,2,0,1:T(8,128)S(1)} %bitcast.121) | data formatting | bytes 16777216 | tf_op jit(solution)/shard_map/transpose | solution.py:52
  186.0 0.6 copy-done.11
  186.6 0.6 gather_fusion
  187.3 1.1 select_bitcast_fusion.1
  188.5 21.2 %reduce-scatter.5.cloned.1.call-done = f32[16,256,256]{2,1,0:T(8,128)} async-done(((f32[32,256,256]{2,1,0:T(8,128)}), f32[16,256,256]{2,1,0:T(8,128)}) %reduce-scatter.5.cloned.1.call-update) | async-done | bytes 4194320 | tf_op jit(solution)/shard_map/reduce_scatter | solution.py:53
  209.7 0.1 reshape.275
  209.8 0.1 fusion.57
  209.9 73.9 %all-gather.5.cloned.1.call-done = bf16[2,16,128,1024]{3,2,0,1:T(8,128)(2,1)} async-done(((bf16[2,2,128,1024]{3,2,0,1:T(8,128)(2,1)}), bf16[2,16,128,1024]{3,2,0,1:T(8,128)(2,1)}) %all-gather.5.cloned.1.call-update) | async-done | bytes 8388624 | tf_op jit(solution)/shard_map/all_gather | solution.py:189
  283.8 8.2 %copy.107 = bf16[2,16,128,1024]{3,2,1,0:T(8,128)(2,1)} copy(bf16[2,16,128,1024]{3,2,0,1:T(8,128)(2,1)} %all-gather.5.cloned.1.call-done) | data formatting | bytes 16777216 | tf_op jit(solution)/shard_map/all_gather | solution.py:189
  292.0 4.1 %gather_fusion.1 = bf16[3,2,128,1024]{3,2,1,0:T(8,128)(2,1)S(1)} fusion(bf16[2,16,128,1024]{3,2,1,0:T(8,128)(2,1)} %copy.107, s32[1024]{0:T(1024)S(1)} %pad_clamp_fusion), kind=kCustom, calls=%fused_computation.1 | custom fusion | bytes 3145740 | tf_op jit(solution)/shard_map/jit(_take)/gather | solution.py:190
  296.1 0.2 select_bitcast_fusion
  296.4 1.3 copy.108
  297.6 1.1 multiply_reduce_fusion
  298.7 0.1 multiply_reduce_fusion.1
  298.8 0.6 broadcast_in_dim.101
  299.5 7.7 %all-to-all-start.3 = ((f32[32,1,16]{2,1,0:T(1,128)}), f32[32,1,16]{2,1,0:T(1,128)S(1)}, u32[]{:S(2)}, u32[]{:S(2)}) async-start(f32[32,1,16]{2,1,0:T(1,128)} %broadcast_in_dim.101), calls=%async_computation.4 | async-start | bytes 32768 | tf_op jit(solution)/shard_map/all_to_all | solution.py:36
  307.2 1.7 fusion.45
  308.9 5.3 %all-to-all-done.3 = f32[32,1,16]{2,1,0:T(1,128)S(1)} async-done(((f32[32,1,16]{2,1,0:T(1,128)}), f32[32,1,16]{2,1,0:T(1,128)S(1)}, u32[]{:S(2)}, u32[]{:S(2)}) %all-to-all-start.3) | async-done | bytes 2080 | tf_op jit(solution)/shard_map/all_to_all | solution.py:36
  314.1 0.6 reduce_sum.69
  (58 shorter events, 0.4 us)
Async XLA Ops:
  8.0 18.3 %copy-start = (bf16[2,2,128,1024]{3,2,1,0:T(8,128)(2,1)S(1)}, bf16[2,2,128,1024]{3,2,1,0:T(8,128)(2,1)}, u32[]{:S(2)}) copy-start(bf16[2,2,128,1024]{3,2,1,0:T(8,128)(2,1)} %param.18) | copy-start | bytes 3145732
  8.0 106.6 %all-gather.3.cloned.1.call-start = ((), (), s32[]{:S(2)}) async-start(), calls=%async_computation.6 | async-start | bytes 4460544 | tf_op jit(solution)/shard_map/all_gather | solution.py:25
  29.8 61.9 %all-to-all-start.1 = ((bf16[2,2,128,32,128]{4,2,1,0,3:T(8,128)(2,1)}), bf16[2,2,128,32,128]{4,2,1,0,3:T(8,128)(2,1)}, u32[]{:S(2)}, u32[]{:S(2)}) async-start(bf16[2,2,128,32,128]{4,2,1,0,3:T(8,128)(2,1)} %bitcast.123), calls=%async_computation.1 | async-start | bytes 8388608 | tf_op jit(solution)/shard_map/all_to_all | solution.py:132
  39.3 6.4 %copy-start.7 = (s32[16]{0:T(128)S(1)}, s32[16]{0:T(128)}, u32[]{:S(2)}) copy-start(s32[16]{0:T(128)} %param.20) | copy-start | bytes 196
  39.3 6.5 %copy-start.3 = (s32[16,32]{1,0:T(8,128)S(1)}, s32[16,32]{1,0:T(8,128)}, u32[]{:S(2)}) copy-start(s32[16,32]{1,0:T(8,128)} %param.19) | copy-start | bytes 6148
  39.3 6.7 %copy-start.8 = (s32[16]{0:T(128)S(1)}, s32[16]{0:T(128)}, u32[]{:S(2)}) copy-start(s32[16]{0:T(128)} %param.21) | copy-start | bytes 196
  96.6 22.1 %copy-start.10 = (bf16[8192,64]{0,1:T(8,128)(2,1)S(1)}, bf16[8192,64]{0,1:T(8,128)(2,1)}, u32[]{:S(2)}) copy-start(bf16[8192,64]{0,1:T(8,128)(2,1)} %param.15) | copy-start | bytes 3145732
  123.4 27.7 %all-to-all-start.2 = ((bf16[32,64,256]{2,1,0:T(8,128)(2,1)}), bf16[32,64,256]{2,1,0:T(8,128)(2,1)}, u32[]{:S(2)}, u32[]{:S(2)}) async-start(bf16[32,64,256]{2,1,0:T(8,128)(2,1)} %broadcast_in_dim.97), calls=%async_computation.2 | async-start | bytes 2097152 | tf_op jit(solution)/shard_map/all_to_all | solution.py:36
  128.9 80.7 %reduce-scatter.5.cloned.1.call-start = ((), (), s32[]{:S(2)}) async-start(), calls=%async_computation.7 | async-start | bytes 12582912 | tf_op jit(solution)/shard_map/reduce_scatter | solution.py:53
  143.4 7.6 %copy-start.6 = (f32[256]{0:T(256)}, f32[256]{0:T(256)S(1)}, u32[]{:S(2)}) copy-start(f32[256]{0:T(256)S(1)} %get-tuple-element.36) | copy-start | bytes 3076
  151.0 3.1 copy-start.5
  157.4 7.5 %copy-start.1 = (f32[256,8192]{1,0:T(8,128)S(1)}, f32[256,8192]{1,0:T(8,128)}, u32[]{:S(2)}) copy-start(f32[256,8192]{1,0:T(8,128)} %get-tuple-element.37) | copy-start | bytes 25165828
  157.4 7.5 %copy-start.4 = (f32[256]{0:T(256)S(1)}, f32[256]{0:T(256)}, u32[]{:S(2)}) copy-start(f32[256]{0:T(256)} %max.34) | copy-start | bytes 3076
  157.4 15.1 %slice-start = ((s8[8388608]{0:T(1024)(128)(4,1)}), s8[4194304]{0:T(1024)(128)(4,1)S(1)}, s32[]{:S(2)}) async-start(s8[8388608]{0:T(1024)(128)(4,1)} %bitcast.125), calls=%async_computation.10 | async-start | bytes 8388608
  164.9 7.6 %slice-start.1 = ((s8[8388608]{0:T(1024)(128)(4,1)}), s8[4194304]{0:T(1024)(128)(4,1)S(1)}, s32[]{:S(2)}) async-start(s8[8388608]{0:T(1024)(128)(4,1)} %bitcast.125), calls=%async_computation.11 | async-start | bytes 8388608
  164.9 7.6 %copy-start.2 = (bf16[1,32,2,128,1,128]{5,3,2,1,4,0:T(8,128)(2,1)S(1)}, bf16[1,32,2,128,1,128]{5,3,2,1,4,0:T(8,128)(2,1)}, u32[]{:S(2)}) copy-start(bf16[1,32,2,128,1,128]{5,3,2,1,4,0:T(8,128)(2,1)} %get-tuple-element.24) | copy-start | bytes 6291460
  185.9 0.7 copy-start.11
  185.9 97.8 %all-gather.5.cloned.1.call-start = ((), (), s32[]{:S(2)}) async-start(), calls=%async_computation.8 | async-start | bytes 9437184 | tf_op jit(solution)/shard_map/all_gather | solution.py:189
  187.2 22.5 %copy-start.12 = (bf16[256]{0:T(256)(128)(2,1)S(1)}, bf16[256]{0:T(256)(128)(2,1)}, u32[]{:S(2)}) copy-start(bf16[256]{0:T(256)(128)(2,1)} %param.17) | copy-start | bytes 1540
  187.2 22.5 %copy-start.13 = (s32[3]{0:T(128)S(1)}, s32[3]{0:T(128)}, u32[]{:S(2)}) copy-start(s32[3]{0:T(128)} %param.23) | copy-start | bytes 40
  187.2 22.6 %copy-start.9 = (s32[16]{0:T(128)S(1)}, s32[16]{0:T(128)}, u32[]{:S(2)}) copy-start(s32[16]{0:T(128)} %param.21) | copy-start | bytes 196
  188.4 109.2 %reduce-scatter.7.cloned.1.call-start = ((), (), s32[]{:S(2)}) async-start(), calls=%async_computation.9 | async-start | bytes 4456448
  299.5 14.7 %all-to-all-start.3 = ((f32[32,1,16]{2,1,0:T(1,128)}), f32[32,1,16]{2,1,0:T(1,128)S(1)}, u32[]{:S(2)}, u32[]{:S(2)}) async-start(f32[32,1,16]{2,1,0:T(1,128)} %broadcast_in_dim.101), calls=%async_computation.4 | async-start | bytes 32768 | tf_op jit(solution)/shard_map/all_to_all | solution.py:36
Sparse Core Ops, SparseCore 0:
  26.4 88.1 all-gather.2
  186.1 23.5 reduce-scatter.4
  213.3 82.5 reduce-scatter.6
Sparse Core Ops, SparseCore 1:
  188.8 94.9 all-gather.4
where the time goes:
time: 323 us; the launch traced here: 322 us
  waiting for transfers between devices  164 us (51%)
  matrix products  40.3 us (12%)
  local copies, waits for them, and re-layouts  39.9 us (12%)
  starting transfers between devices  23 us (7%)
  other arithmetic  22.2 us (7%)
  blocking collectives  16.9 us (5%)
  between operations  15.5 us (5%)
    all_gather x1, waiting for transfers between devices, local(): gathered = lax.all_gather(gathered_elements, 'group', axis=1, tiled=True)  73.9 us
    all_to_all x1, waiting for transfers between devices, local(): lax.all_to_all(spread, MP, split_axis=3, concat_axis=1, tiled=True)  45.6 us
    reduce_scatter x1, waiting for transfers between devices, scatter_pairs(): tiles = lax.psum_scatter(tiles, core, scatter_dimension=0, tiled=True)  21.2 us
    all_gather x1, waiting for transfers between devices, sent_together(): lax.all_gather(both, axis, axis=dim, tiled=True)  18.1 us
    all_to_all x1, blocking collectives, local(): lax.all_to_all(option_latent_states, 'group', split_axis=0, concat_axis=0...  16.9 us
    dot_general x2, matrix products, local(): jnp.einsum('rd,pd->rp', my_queries[:, head_index], path_keys, preferred_e...  15 us
    all_to_all x2, starting transfers between devices, from_everyone(): return lax.all_to_all(copies, axis, split_axis=0, concat_axis=0, tiled=True)  13.2 us
    dot_general x2, matrix products, local(): jnp.dot(head_mass.astype(jnp.bfloat16), path_values, preferred_element_ty...  11.2 us
  transfers between devices with their start and end apart: 7, of which 5 were waited for; matrix products, arithmetic and copies ran while one was open for 17% of the time, Pallas kernels for 0%

commit v1 on v0

--- a/solution.py
+++ b/solution.py
@@ -14,6 +14,28 @@
 GROUP_MP = ("group", "mp_0", "mp_1", "mp_2")
 epsilon = 1e-06
 masked_value = -1e30
+
+
+def in_order_2(tiles, dim):
+    tiles = jnp.moveaxis(tiles, 0, dim)
+    shape = tiles.shape
+    return tiles.reshape(*shape[:dim], shape[dim] * shape[dim + 1], *shape[dim + 2 :])
+
+
+def ring_gather(value, axis, dim):
+    size = lax.axis_size(axis)
+    pairs = [(i, (i + 1) % size) for i in range(size)]
+    back = [(b, a) for a, b in pairs]
+    lower, upper = ([], [])
+    for hop in range(size - 1):
+        if hop % 2 == 0:
+            lower.append(lax.ppermute(lower[-1] if lower else value, axis, pairs))
+        else:
+            upper.append(lax.ppermute(upper[-1] if upper else value, axis, back))
+    parts = jnp.stack([*lower[::-1], value, *upper])
+    shift = lax.axis_index(axis) - len(lower)
+    parts = parts[(jnp.arange(size) - shift) % size]
+    return in_order_2(parts, dim)
 
 
 def sent_together(arrays, axis, dim, along):
@@ -186,7 +208,7 @@
     )
     rewards = over_copies(partial_reward, MP)
     gathered_elements = jnp.take(shared_trie_memo, retained_pages, axis=1)
-    gathered = lax.all_gather(gathered_elements, "group", axis=1, tiled=True)
+    gathered = ring_gather(gathered_elements, "group", 1)
     expanded = jnp.take(gathered, growth_place_mapping, axis=1)
     return (scored_rows, rewards, expanded)
 

time: 323 us -> 373 us (1.15)
  local copies, waits for them, and re-layouts: 39.9 us -> 60.8 us
  waiting for transfers between devices: 164 us -> 182 us
  starting transfers between devices: 23 us -> 35.6 us
    ppermute x0 -> x7, waiting for transfers between devices: none -> 89.1 us  [the longest x4 89.1 us: ring_gather(): lower.append(lax.ppermute(lower[-1] if lower else value, axis, pairs))]
    all_gather x1 -> x0, waiting for transfers between devices: 73.9 us -> none  [local(): gathered = lax.all_gather(gathered_elements, 'group', axis=1, tiled=True)]
    unnamed x33 -> x41, local copies, waits for them, and re-layouts: 1.93 us -> 13.8 us
    ppermute x0 -> x7, starting transfers between devices: none -> 9.26 us  [the longest x3 8.12 us: ring_gather(): upper.append(lax.ppermute(upper[-1] if upper else value, axis, back))]
    all_gather x1 -> x0, local copies, waits for them, and re-layouts: 8.24 us -> none  [local(): gathered = lax.all_gather(gathered_elements, 'group', axis=1, tiled=True)]
    transpose x0 -> x1, local copies, waits for them, and re-layouts: none -> 8.21 us  [in_order_2(): tiles = jnp.moveaxis(tiles, 0, dim)]
    gather x0 -> x1, local copies, waits for them, and re-layouts: none -> 8.06 us  [ring_gather(): parts = parts[(jnp.arange(size) - shift) % size]]
  transfers between devices with their start and end apart: 7 -> 13, of which waited for: 5 -> 8; matrix products, arithmetic and copies ran while one was open for 17% -> 21% of each run, Pallas kernels for 0% -> 0%
where the time goes in v1:
time: 373 us; the launch traced here: 372 us
  waiting for transfers between devices  182 us (49%)
  local copies, waits for them, and re-layouts  60.8 us (16%)
  matrix products  40.3 us (11%)
  starting transfers between devices  35.6 us (10%)
  other arithmetic  22.5 us (6%)
  blocking collectives  16.9 us (5%)
  between operations  14.1 us (4%)
    ppermute x4, waiting for transfers between devices, ring_gather(): lower.append(lax.ppermute(lower[-1] if lower else value, axis, pairs))  89.1 us
    all_to_all x1, waiting for transfers between devices, local(): lax.all_to_all(spread, MP, split_axis=3, concat_axis=1, tiled=True)  44.1 us
    reduce_scatter x1, waiting for transfers between devices, scatter_pairs(): tiles = lax.psum_scatter(tiles, core, scatter_dimension=0, tiled=True)  23.6 us
    all_gather x1, waiting for transfers between devices, sent_together(): lax.all_gather(both, axis, axis=dim, tiled=True)  19.5 us
    all_to_all x1, blocking collectives, local(): lax.all_to_all(option_latent_states, 'group', split_axis=0, concat_axis=0...  16.9 us
    all_to_all x2, starting transfers between devices, from_everyone(): return lax.all_to_all(copies, axis, split_axis=0, concat_axis=0, tiled=True)  16.5 us
    dot_general x2, matrix products, local(): jnp.einsum('rd,pd->rp', my_queries[:, head_index], path_keys, preferred_e...  15 us
    unnamed x41, local copies, waits for them, and re-layouts  13.8 us
  transfers between devices with their start and end apart: 13, of which 8 were waited for; matrix products, arithmetic and copies ran while one was open for 21% of the time, Pallas kernels for 0%

profile of v1, /device:TPU:1, one launch (start us, length us, event | category | flops | bytes accessed | tf_op | source)
XLA Modules:
  0.0 371.9 jit_solution(225709160765624638)
XLA Ops:
  7.2 16.9 %all_to_all.38 = bf16[8,32,256]{2,1,0:T(8,128)(2,1)S(1)} all-to-all(bf16[8,32,256]{2,1,0:T(8,128)(2,1)} %bitcast.165), channel_id=1, replica_groups=mesh['group'=8,'mp_0'=4,'mp_1'=4,'mp_2'=2] {'group'}, dimensions={0} | all-to-all | bytes 262144 | tf_op jit(solution)/shard_map/all_to_all | solution.py:100
  24.1 1.3 pad_maximum_fusion
  25.5 0.3 copy_bitcast_fusion.1
  25.8 3.2 broadcast_in_dim.99
  29.0 9.6 %all-to-all-start.1 = ((bf16[2,2,128,32,128]{4,2,1,0,3:T(8,128)(2,1)}), bf16[2,2,128,32,128]{4,2,1,0,3:T(8,128)(2,1)}, u32[]{:S(2)}, u32[]{:S(2)}) async-start(bf16[2,2,128,32,128]{4,2,1,0,3:T(8,128)(2,1)} %bitcast.147), calls=%async_computation.1 | async-start | bytes 8388608 | tf_op jit(solution)/shard_map/all_to_all | solution.py:154
  38.6 6.3 %copy.104 = bf16[8192,128,2]{1,0,2:T(8,128)(2,1)} copy(bf16[8192,128,2]{0,1,2:T(8,128)(2,1)} %bitcast.157) | data formatting | bytes 8388608 | tf_op jit(solution)/shard_map/jrd,jdf->rf/dot_general | solution.py:195
  45.1 0.2 fusion.48
  45.5 44.1 %all-to-all-done.1 = bf16[2,2,128,32,128]{4,2,1,0,3:T(8,128)(2,1)} async-done(((bf16[2,2,128,32,128]{4,2,1,0,3:T(8,128)(2,1)}), bf16[2,2,128,32,128]{4,2,1,0,3:T(8,128)(2,1)}, u32[]{:S(2)}, u32[]{:S(2)}) %all-to-all-start.1) | async-done | bytes 4194336 | tf_op jit(solution)/shard_map/all_to_all | solution.py:154
  89.6 2.5 copy.136
  92.1 2.3 fusion.67
  94.4 19.5 %all-gather.2.cloned.1.call-done = bf16[257,8192]{1,0:T(8,128)(2,1)} async-done(((bf16[257,256]{1,0:T(8,128)(2,1)}), bf16[257,8192]{1,0:T(8,128)(2,1)}) %all-gather.2.cloned.1.call-update) | async-done | bytes 4210704 | tf_op jit(solution)/shard_map/all_gather | solution.py:47
  113.9 3.1 fusion.3
  117.0 0.9 slice_convert_fusion
  117.9 3.6 fusion.40
  121.5 1.1 broadcast_in_dim.102
  122.6 5.5 %all-to-all-start.2 = ((bf16[32,64,256]{2,1,0:T(8,128)(2,1)}), bf16[32,64,256]{2,1,0:T(8,128)(2,1)}, u32[]{:S(2)}, u32[]{:S(2)}) async-start(bf16[32,64,256]{2,1,0:T(8,128)(2,1)} %broadcast_in_dim.102), calls=%async_computation.2 | async-start | bytes 2097152 | tf_op jit(solution)/shard_map/all_to_all | solution.py:58
  128.3 5.4 %fusion.25 = bf16[256,256]{0,1:T(8,128)(2,1)S(1)} fusion(bf16[8192,256]{1,0:T(8,128)(2,1)} %param.14, f32[8192]{0:T(1024)S(1)} %bitcast.173, bf16[257,8192]{1,0:T(8,128)(2,1)} %all-gather.2.cloned.1.call-done, f32[256]{0:T(256)S(1)} %add_rsqrt_fusion), kind=kOutput, calls=%fused_computation.32 | convolution fusion | flops 1080164352 | bytes 8553472 | tf_op jit(solution)/shard_map/dot_general | solution.py:112
  133.9 0.7 reshape.326
  134.5 0.6 broadcast_in_dim.97
  135.2 7.5 %fusion.71 = (f32[256]{0:T(256)S(1)}, f32[256,8192]{1,0:T(8,128)}) fusion(bf16[8192,128]{1,0:T(8,128)(2,1)} %bitcast.160, bf16[256,2,128]{0,2,1:T(8,128)(2,1)S(1)} %bitcast.166, pred[32,8,64,128]{3,2,1,0:T(32,128)(4,1)S(1)} %bitcast.152), kind=kOutput, calls=%fused_computation.108 | convolution fusion | flops 543162112 | bytes 12649472 | tf_op jit(solution)/shard_map/rd,pd->rp/dot_general | solution.py:166
  142.7 7.5 %fusion.69 = (f32[256]{0:T(256)S(1)}, f32[256,8192]{1,0:T(8,128)}) fusion(bf16[8192,128]{1,0:T(8,128)(2,1)} %bitcast.161, bf16[256,2,128]{0,2,1:T(8,128)(2,1)S(1)} %bitcast.167, pred[32,8,64,128]{3,2,1,0:T(32,128)(4,1)S(1)} %bitcast.153), kind=kOutput, calls=%fused_computation.106 | convolution fusion | flops 543162112 | bytes 12649472 | tf_op jit(solution)/shard_map/rd,pd->rp/dot_general | solution.py:166
  150.3 0.9 constant_dynamic-slice_fusion
  151.2 0.7 copy.95
  151.9 1.4 fusion.70
  153.4 0.6 squeeze.20
  154.0 1.2 max.34
  155.2 0.6 squeeze.22
  155.9 0.7 max.35
  156.5 7.5 %fusion.28 = f32[1,256,128]{2,1,0:T(8,128)} fusion(bf16[8192,128]{1,0:T(8,128)(2,1)} %bitcast.158, f32[256,8192]{1,0:T(8,128)} %get-tuple-element.37, f32[256]{0:T(256)} %max.34, pred[32,8,64,128]{3,2,1,0:T(32,128)(4,1)S(1)} %bitcast.154), kind=kOutput, calls=%fused_computation.33 | convolution fusion | flops 543162368 | bytes 12715008 | tf_op jit(solution)/shard_map/dot_general | solution.py:178
  164.1 7.6 %fusion.4 = (f32[256]{0:T(256)}, f32[256]{0:T(256)}) fusion(f32[256,8192]{1,0:T(8,128)S(1)} %copy-done.1, f32[256]{0:T(256)S(1)} %copy-done.5, pred[32,8,64,128]{3,2,1,0:T(32,128)(4,1)S(1)} %bitcast.155, f32[256,8192]{1,0:T(8,128)} %get-tuple-element.33, f32[256]{0:T(256)S(1)} %max.35), kind=kLoop, calls=%fused_computation.13 | loop fusion | flops 12582400 | bytes 18878464 | tf_op jit(solution)/shard_map/reduce_sum | solution.py:180
  171.7 3.7 %fusion.31 = f32[1,256,128]{2,1,0:T(8,128)} fusion(bf16[8192,128]{1,0:T(8,128)(2,1)S(1)} %bitcast.159, f32[256,8192]{1,0:T(8,128)S(1)} %bitcast.151, f32[256]{0:T(256)S(1)} %max.35, pred[32,8,64,128]{3,2,1,0:T(32,128)(4,1)S(1)} %bitcast.156), kind=kOutput, calls=%fused_computation.34 | convolution fusion | flops 543162368 | bytes 12715008 | tf_op jit(solution)/shard_map/dot_general | solution.py:178
  175.7 0.2 convolution_bitcast_fusion
  176.0 0.7 maximum_add_fusion.1
  176.7 1.1 fusion.45
  177.8 3.5 fusion.52
  181.3 3.8 %copy.106 = f32[2,16,256,256]{3,2,1,0:T(8,128)} copy(f32[2,16,256,256]{3,2,0,1:T(8,128)S(1)} %bitcast.144) | data formatting | bytes 16777216 | tf_op jit(solution)/shard_map/transpose | solution.py:74
  185.2 23.6 %reduce-scatter.5.cloned.1.call-done = f32[16,256,256]{2,1,0:T(8,128)} async-done(((f32[32,256,256]{2,1,0:T(8,128)}), f32[16,256,256]{2,1,0:T(8,128)}) %reduce-scatter.5.cloned.1.call-update) | async-done | bytes 4194320 | tf_op jit(solution)/shard_map/reduce_scatter | solution.py:75
  208.9 0.6 gather_fusion
  209.7 1.1 collective-permute-start
  210.8 24.8 %collective-permute-done = bf16[2,2,128,1024]{3,2,0,1:T(8,128)(2,1)S(1)} collective-permute-done((bf16[2,2,128,1024]{3,2,0,1:T(8,128)(2,1)S(1)}, bf16[2,2,128,1024]{3,2,0,1:T(8,128)(2,1)S(1)}, u32[]{:S(2)}, u32[]{:S(2)}) %collective-permute-start) | collective-permute-done | bytes 1048608 | tf_op jit(solution)/shard_map/ppermute | solution.py:32
  235.6 2.7 collective-permute-start.4
  238.3 22.3 %collective-permute-done.1 = bf16[2,2,128,1024]{3,2,0,1:T(8,128)(2,1)} collective-permute-done((bf16[2,2,128,1024]{3,2,0,1:T(8,128)(2,1)S(1)}, bf16[2,2,128,1024]{3,2,0,1:T(8,128)(2,1)}, u32[]{:S(2)}, u32[]{:S(2)}) %collective-permute-start.1) | collective-permute-done | bytes 1048608 | tf_op jit(solution)/shard_map/ppermute | solution.py:32
  260.6 2.7 collective-permute-start.5
  263.3 21.5 %collective-permute-done.2 = bf16[2,2,128,1024]{3,2,0,1:T(8,128)(2,1)} collective-permute-done((bf16[2,2,128,1024]{3,2,0,1:T(8,128)(2,1)}, bf16[2,2,128,1024]{3,2,0,1:T(8,128)(2,1)}, u32[]{:S(2)}, u32[]{:S(2)}) %collective-permute-start.2) | collective-permute-done | bytes 1048608 | tf_op jit(solution)/shard_map/ppermute | solution.py:32
  285.1 2.7 collective-permute-start.6
  287.8 20.5 %collective-permute-done.3 = bf16[2,2,128,1024]{3,2,0,1:T(8,128)(2,1)} collective-permute-done((bf16[2,2,128,1024]{3,2,0,1:T(8,128)(2,1)}, bf16[2,2,128,1024]{3,2,0,1:T(8,128)(2,1)}, u32[]{:S(2)}, u32[]{:S(2)}) %collective-permute-start.3) | collective-permute-done | bytes 1048608 | tf_op jit(solution)/shard_map/ppermute | solution.py:32
  308.3 2.3 bitcast_dynamic-update-slice_fusion.6
  310.6 2.3 bitcast_dynamic-update-slice_fusion.5
  312.9 2.3 bitcast_dynamic-update-slice_fusion.4
  315.2 2.3 bitcast_dynamic-update-slice_fusion.3
  317.5 1.3 fusion.43
  318.8 2.3 bitcast_dynamic-update-slice_fusion.2
  321.1 1.1 bitcast_dynamic-update-slice_fusion.1
  322.2 1.1 bitcast_dynamic-update-slice_fusion
  323.3 8.1 %gather_fusion.1 = bf16[8,2,2,128,1024]{4,3,1,2,0:T(8,128)(2,1)} fusion(bf16[8,2,2,128,1024]{4,3,1,2,0:T(8,128)(2,1)} %bitcast_dynamic-update-slice_fusion, s32[1024]{0:T(1024)S(1)} %pad_clamp_fusion.1), kind=kCustom, calls=%fused_computation.1 | custom fusion | bytes 16777248 | tf_op jit(solution)/shard_map/gather | solution.py:37
  331.3 8.2 %copy.108 = bf16[2,8,2,128,1024]{4,3,2,1,0:T(8,128)(2,1)} copy(bf16[2,8,2,128,1024]{4,3,0,2,1:T(8,128)(2,1)} %bitcast.145) | data formatting | bytes 16777216 | tf_op jit(solution)/shard_map/transpose | solution.py:20
  339.5 4.0 %gather_fusion.2 = bf16[3,2,128,1024]{3,2,1,0:T(8,128)(2,1)S(1)} fusion(bf16[2,16,128,1024]{3,2,1,0:T(8,128)(2,1)} %bitcast.149, s32[1024]{0:T(1024)S(1)} %pad_clamp_fusion), kind=kCustom, calls=%fused_computation.2 | custom fusion | bytes 3145740 | tf_op jit(solution)/shard_map/jit(_take)/gather | solution.py:212
  343.8 1.3 copy.109
  345.0 1.1 multiply_reduce_fusion
  346.2 0.6 broadcast_in_dim.106
  346.9 11.0 %all-to-all-start.3 = ((f32[32,1,16]{2,1,0:T(1,128)}), f32[32,1,16]{2,1,0:T(1,128)S(1)}, u32[]{:S(2)}, u32[]{:S(2)}) async-start(f32[32,1,16]{2,1,0:T(1,128)} %broadcast_in_dim.106), calls=%async_computation.4 | async-start | bytes 32768 | tf_op jit(solution)/shard_map/all_to_all | solution.py:58
  357.9 1.7 fusion.46
  359.6 5.3 %all-to-all-done.3 = f32[32,1,16]{2,1,0:T(1,128)S(1)} async-done(((f32[32,1,16]{2,1,0:T(1,128)}), f32[32,1,16]{2,1,0:T(1,128)S(1)}, u32[]{:S(2)}, u32[]{:S(2)}) %all-to-all-start.3) | async-done | bytes 2080 | tf_op jit(solution)/shard_map/all_to_all | solution.py:58
  364.9 0.6 reduce_sum.69
  (82 shorter events, 2.1 us)
Async XLA Ops:
  7.2 18.3 %copy-start = (bf16[2,2,128,1024]{3,2,1,0:T(8,128)(2,1)S(1)}, bf16[2,2,128,1024]{3,2,1,0:T(8,128)(2,1)}, u32[]{:S(2)}) copy-start(bf16[2,2,128,1024]{3,2,1,0:T(8,128)(2,1)} %param.18) | copy-start | bytes 3145732
  7.2 106.7 %all-gather.2.cloned.1.call-start = ((), (), s32[]{:S(2)}) async-start(), calls=%async_computation.6 | async-start | bytes 4460544 | tf_op jit(solution)/shard_map/all_gather | solution.py:47
  29.0 16.0 %copy-start.8 = (s32[16]{0:T(128)S(1)}, s32[16]{0:T(128)}, u32[]{:S(2)}) copy-start(s32[16]{0:T(128)} %param.20) | copy-start | bytes 196
  29.0 16.0 %copy-start.4 = (s32[16,32]{1,0:T(8,128)S(1)}, s32[16,32]{1,0:T(8,128)}, u32[]{:S(2)}) copy-start(s32[16,32]{1,0:T(8,128)} %param.19) | copy-start | bytes 6148
  29.0 16.3 %copy-start.9 = (s32[16]{0:T(128)S(1)}, s32[16]{0:T(128)}, u32[]{:S(2)}) copy-start(s32[16]{0:T(128)} %param.21) | copy-start | bytes 196
  29.0 60.5 %all-to-all-start.1 = ((bf16[2,2,128,32,128]{4,2,1,0,3:T(8,128)(2,1)}), bf16[2,2,128,32,128]{4,2,1,0,3:T(8,128)(2,1)}, u32[]{:S(2)}, u32[]{:S(2)}) async-start(bf16[2,2,128,32,128]{4,2,1,0,3:T(8,128)(2,1)} %bitcast.147), calls=%async_computation.1 | async-start | bytes 8388608 | tf_op jit(solution)/shard_map/all_to_all | solution.py:154
  92.0 25.9 %copy-start.11 = (bf16[8192,64]{0,1:T(8,128)(2,1)S(1)}, bf16[8192,64]{0,1:T(8,128)(2,1)}, u32[]{:S(2)}) copy-start(bf16[8192,64]{0,1:T(8,128)(2,1)} %param.15) | copy-start | bytes 3145732
  122.6 27.7 %all-to-all-start.2 = ((bf16[32,64,256]{2,1,0:T(8,128)(2,1)}), bf16[32,64,256]{2,1,0:T(8,128)(2,1)}, u32[]{:S(2)}, u32[]{:S(2)}) async-start(bf16[32,64,256]{2,1,0:T(8,128)(2,1)} %broadcast_in_dim.102), calls=%async_computation.2 | async-start | bytes 2097152 | tf_op jit(solution)/shard_map/all_to_all | solution.py:58
  128.1 80.7 %reduce-scatter.5.cloned.1.call-start = ((), (), s32[]{:S(2)}) async-start(), calls=%async_computation.7 | async-start | bytes 12582912 | tf_op jit(solution)/shard_map/reduce_scatter | solution.py:75
  142.6 7.6 %copy-start.7 = (f32[256]{0:T(256)}, f32[256]{0:T(256)S(1)}, u32[]{:S(2)}) copy-start(f32[256]{0:T(256)S(1)} %get-tuple-element.36) | copy-start | bytes 3076
  150.2 3.1 copy-start.6
  156.5 7.5 %copy-start.1 = (f32[256,8192]{1,0:T(8,128)S(1)}, f32[256,8192]{1,0:T(8,128)}, u32[]{:S(2)}) copy-start(f32[256,8192]{1,0:T(8,128)} %get-tuple-element.37) | copy-start | bytes 25165828
  156.5 7.5 %copy-start.5 = (f32[256]{0:T(256)S(1)}, f32[256]{0:T(256)}, u32[]{:S(2)}) copy-start(f32[256]{0:T(256)} %max.34) | copy-start | bytes 3076
  156.5 15.1 %slice-start = ((s8[8388608]{0:T(1024)(128)(4,1)}), s8[4194304]{0:T(1024)(128)(4,1)S(1)}, s32[]{:S(2)}) async-start(s8[8388608]{0:T(1024)(128)(4,1)} %bitcast.150), calls=%async_computation.9 | async-start | bytes 8388608
  164.1 7.6 %slice-start.1 = ((s8[8388608]{0:T(1024)(128)(4,1)}), s8[4194304]{0:T(1024)(128)(4,1)S(1)}, s32[]{:S(2)}) async-start(s8[8388608]{0:T(1024)(128)(4,1)} %bitcast.150), calls=%async_computation.10 | async-start | bytes 8388608
  164.1 7.6 %copy-start.2 = (bf16[1,32,2,128,1,128]{5,3,2,1,4,0:T(8,128)(2,1)S(1)}, bf16[1,32,2,128,1,128]{5,3,2,1,4,0:T(8,128)(2,1)}, u32[]{:S(2)}) copy-start(bf16[1,32,2,128,1,128]{5,3,2,1,4,0:T(8,128)(2,1)} %get-tuple-element.24) | copy-start | bytes 6291460
  185.1 23.8 %copy-start.12 = (s32[2]{0:T(128)S(1)}, s32[2]{0:T(128)}, u32[]{:S(2)}) copy-start(s32[2]{0:T(128)} %param.22) | copy-start | bytes 28
  185.1 99.9 %copy-start.13 = (bf16[256]{0:T(256)(128)(2,1)S(1)}, bf16[256]{0:T(256)(128)(2,1)}, u32[]{:S(2)}) copy-start(bf16[256]{0:T(256)(128)(2,1)} %param.17) | copy-start | bytes 1540
  185.1 99.9 %copy-start.14 = (s32[3]{0:T(128)S(1)}, s32[3]{0:T(128)}, u32[]{:S(2)}) copy-start(s32[3]{0:T(128)} %param.23) | copy-start | bytes 40
  185.1 99.9 %copy-start.10 = (s32[16]{0:T(128)S(1)}, s32[16]{0:T(128)}, u32[]{:S(2)}) copy-start(s32[16]{0:T(128)} %param.21) | copy-start | bytes 196
  185.1 159.9 %reduce-scatter.7.cloned.1.call-start = ((), (), s32[]{:S(2)}) async-start(), calls=%async_computation.8 | async-start | bytes 4456448
  209.7 25.9 %collective-permute-start = (bf16[2,2,128,1024]{3,2,0,1:T(8,128)(2,1)S(1)}, bf16[2,2,128,1024]{3,2,0,1:T(8,128)(2,1)S(1)}, u32[]{:S(2)}, u32[]{:S(2)}) collective-permute-start(bf16[2,2,128,1024]{3,2,0,1:T(8,128)(2,1)S(1)} %bitcast_select_fusion.1), channel_id=1, source_target_pairs={{0,32},{32,64},{64,96},{96,128},{128,160},{160,192},{192,224},{224... | collective-permute-start | bytes 3145736 | tf_op jit(solution)/shard_map/ppermute | solution.py:32
  235.6 2.7 copy-start.3
  235.6 25.0 %collective-permute-start.1 = (bf16[2,2,128,1024]{3,2,0,1:T(8,128)(2,1)S(1)}, bf16[2,2,128,1024]{3,2,0,1:T(8,128)(2,1)}, u32[]{:S(2)}, u32[]{:S(2)}) collective-permute-start(bf16[2,2,128,1024]{3,2,0,1:T(8,128)(2,1)S(1)} %collective-permute-done), channel_id=1, source_target_pairs={{0,32},{32,64},{64,96},{96,128},{128,160},{160,192},{192,224},{224... | collective-permute-start | bytes 3145736 | tf_op jit(solution)/shard_map/ppermute | solution.py:32
  235.6 25.0 %collective-permute-start.4 = (bf16[2,2,128,1024]{3,2,0,1:T(8,128)(2,1)S(1)}, bf16[2,2,128,1024]{3,2,0,1:T(8,128)(2,1)}, u32[]{:S(2)}, u32[]{:S(2)}) collective-permute-start(bf16[2,2,128,1024]{3,2,0,1:T(8,128)(2,1)S(1)} %bitcast_select_fusion.1), channel_id=1, source_target_pairs={{32,0},{64,32},{96,64},{128,96},{160,128},{192,160},{224,192},{0,2... | collective-permute-start | bytes 3145736 | tf_op jit(solution)/shard_map/ppermute | solution.py:34
  260.6 24.3 %collective-permute-start.2 = (bf16[2,2,128,1024]{3,2,0,1:T(8,128)(2,1)}, bf16[2,2,128,1024]{3,2,0,1:T(8,128)(2,1)}, u32[]{:S(2)}, u32[]{:S(2)}) collective-permute-start(bf16[2,2,128,1024]{3,2,0,1:T(8,128)(2,1)} %collective-permute-done.1), channel_id=1, source_target_pairs={{0,32},{32,64},{64,96},{96,128},{128,160},{160,192},{192,224},{224... | collective-permute-start | bytes 3145736 | tf_op jit(solution)/shard_map/ppermute | solution.py:32
  260.6 24.5 %collective-permute-start.5 = (bf16[2,2,128,1024]{3,2,0,1:T(8,128)(2,1)}, bf16[2,2,128,1024]{3,2,0,1:T(8,128)(2,1)S(1)}, u32[]{:S(2)}, u32[]{:S(2)}) collective-permute-start(bf16[2,2,128,1024]{3,2,0,1:T(8,128)(2,1)} %collective-permute-done.4), channel_id=1, source_target_pairs={{32,0},{64,32},{96,64},{128,96},{160,128},{192,160},{224,192},{0,2... | collective-permute-start | bytes 3145736 | tf_op jit(solution)/shard_map/ppermute | solution.py:34
  284.9 23.5 %collective-permute-start.3 = (bf16[2,2,128,1024]{3,2,0,1:T(8,128)(2,1)}, bf16[2,2,128,1024]{3,2,0,1:T(8,128)(2,1)}, u32[]{:S(2)}, u32[]{:S(2)}) collective-permute-start(bf16[2,2,128,1024]{3,2,0,1:T(8,128)(2,1)} %collective-permute-done.2), channel_id=1, source_target_pairs={{0,32},{32,64},{64,96},{96,128},{128,160},{160,192},{192,224},{224... | collective-permute-start | bytes 3145736 | tf_op jit(solution)/shard_map/ppermute | solution.py:32
  285.1 37.1 %collective-permute-start.6 = (bf16[2,2,128,1024]{3,2,0,1:T(8,128)(2,1)S(1)}, bf16[2,2,128,1024]{3,2,0,1:T(8,128)(2,1)S(1)}, u32[]{:S(2)}, u32[]{:S(2)}) collective-permute-start(bf16[2,2,128,1024]{3,2,0,1:T(8,128)(2,1)S(1)} %collective-permute-done.5), channel_id=1, source_target_pairs={{32,0},{64,32},{96,64},{128,96},{160,128},{192,160},{224,192},{0,2... | collective-permute-start | bytes 3145736 | tf_op jit(solution)/shard_map/ppermute | solution.py:34
  346.9 18.0 %all-to-all-start.3 = ((f32[32,1,16]{2,1,0:T(1,128)}), f32[32,1,16]{2,1,0:T(1,128)S(1)}, u32[]{:S(2)}, u32[]{:S(2)}) async-start(f32[32,1,16]{2,1,0:T(1,128)} %broadcast_in_dim.106), calls=%async_computation.4 | async-start | bytes 32768 | tf_op jit(solution)/shard_map/all_to_all | solution.py:58
Sparse Core Ops, SparseCore 0:
  25.6 88.2 all-gather.1
  185.3 23.5 reduce-scatter.4
  212.5 82.7 reduce-scatter.6
